TPU v7x, 256 devices: a whole 4x4x8 slice. The times are simulated.
256 devices in a mesh: dp: 64 (over z, x_hi, y), rep: 4 (over x_lo, core).
Axes of the slice: x: 4 (x_hi: 2, x_lo: 2; x = x_hi * 2 + x_lo), y: 4, z: 8, core: 2. Of those that a mesh axis runs over, the one named last changes fastest.
Arguments:
- tokens: bfloat16 [1024, 128, 2048], P(('dp', 'rep')), may hold values from -32 to 32, as said below
- cotangent: bfloat16 [1024, 128, 1024], P(('dp', 'rep')), may hold values from -6 to 6
- projection: bfloat16 [2048, 1536], replicated, may hold values from -0.25 to 0.25
- block_lengths: int32 [256, 4], P(('dp', 'rep')), may hold values from 0 to 128, as said below
- destination: int32 [256], P(('dp', 'rep')), may hold values from -1 to 63, as said below
Outputs:
- direction: float32 [2048, 1536], P(('dp', 'rep'))
Inputs may be any that keep to these rules, and one draw needn't show every extreme that they name: `tokens`: clipped at the range's ends. `block_lengths`: A device's live slots come first, all of length 128 except the last live one, which holds 64 to 128 tokens; later slots have length 0. A device has 1 to 4 live slots, and some device has 4 in every draw. A device has a destination exactly when it has 4 live slots. The destination's dp index differs from the sender's in exactly one bit, the rep index is the same, the receiver has at most 2 live slots, and no device receives from two senders.
All inputs are finite; a program needn't handle non-finite values.
Results may differ from a plain program's by a relative error of at most 0.006.
The roundings to bfloat16 on the way count: a program that leaves them out, or rounds other values in their place, can miss the bound.
Values may be sent and summed in bfloat16 or wider, within the bound.
A program may use at most 128 MiB of HBM per device.

v0:
```python
import math

import jax
import jax.numpy as jnp
from jax import lax
from jax.experimental import pallas as pl
from jax.experimental.pallas import tpu as pltpu
from jax.sharding import Mesh
from jax.sharding import PartitionSpec as P

HS = 256
HEADS = 4
BLOCK = 128
DP_REP = ("dp_0", "dp_1", "dp_2", "rep_0", "rep_1")
REP = ("rep_0", "rep_1")
DP = ("dp_0", "dp_1", "dp_2")
GROUPS = HEADS + 2
D = 2048
MESH = pl.DeviceIdType.MESH
F32 = jnp.float32
BF16 = jnp.bfloat16


def dot(a, b, ca, cb):
    return lax.dot_general(a, b, (((ca,), (cb,)), ((), ())), preferred_element_type=F32)


def attention(at, length, joined, up, comb):
    scale = HS ** (-0.5)

    def heads(ref):
        return jnp.concatenate([ref[at, h * HS : (h + 1) * HS] for h in range(HEADS)], axis=0)

    query = heads(joined)
    keys = joined[at, HEADS * HS : (HEADS + 1) * HS]
    values = joined[at, (HEADS + 1) * HS :]
    shape = (HEADS * BLOCK, BLOCK)
    row = lax.rem(lax.broadcasted_iota(jnp.int32, shape, 0), BLOCK)
    col = lax.broadcasted_iota(jnp.int32, shape, 1)
    allowed = (col <= row) & (col < jnp.broadcast_to(length, shape))
    scores = jnp.where(allowed, dot(query, keys, 1, 1) * scale, -1e30)
    peak = jnp.max(scores, axis=-1, keepdims=True)
    expo = jnp.exp(scores - peak)
    weights = expo / jnp.sum(expo, axis=-1, keepdims=True)
    wide = (HEADS * BLOCK, HS)
    live = lax.rem(lax.broadcasted_iota(jnp.int32, wide, 0), BLOCK) < jnp.broadcast_to(length, wide)
    upstream = jnp.where(live, heads(up).astype(F32), 0.0).astype(BF16)
    probs = weights.astype(BF16)
    grad_values = dot(probs.T, upstream, 1, 0).astype(BF16)
    grad_probs = dot(upstream, values, 1, 1)
    centre = jnp.sum(weights * grad_probs, axis=-1, keepdims=True)
    grad_scores = (weights * (grad_probs - centre) * scale).astype(BF16)
    grad_query = dot(grad_scores, keys, 1, 0).astype(BF16)
    grad_keys = dot(grad_scores.T, query, 1, 0).astype(BF16)
    for h in range(HEADS):
        comb[at, h * HS : (h + 1) * HS] = grad_query[h * BLOCK : (h + 1) * BLOCK]
    comb[at, HEADS * HS : (HEADS + 1) * HS] = grad_keys
    comb[at, (HEADS + 1) * HS :] = grad_values


SLABS = 4
SLAB = D // SLABS


def slab_copy(proj, proj_v, sem, k):
    at = pl.ds(k * SLAB, SLAB)
    return pltpu.make_async_copy(proj.at[at], proj_v.at[at], sem.at[k])


def join(proj, proj_v, sem, x, acc, joined):
    for k in range(SLABS):
        slab_copy(proj, proj_v, sem, k).wait()
        at = slice(k * SLAB, (k + 1) * SLAB)
        part = dot(x[:, at], proj_v[at, :], 1, 0)
        if k == SLABS - 1:
            joined[...] = (acc[...] + part).astype(BF16)
        elif k:
            acc[...] += part
        else:
            acc[...] = part


NZ, NY, NX = 8, 4, 4


def wrap(i, n):
    return lax.rem(i + n, n)


def vote_kernel(info, tok, cot, tok_a, cot_a, tok_b, cot_b, proj, comb01, xt01, out,
                cand_t, cand_c, proj_v, x3, up3, acc3, joined3, comb3, xt3, grad, mail,
                part, wz, wx, wy, rzp0, rzp1, rzm0, rzm1, szp0, szp1, szm0,
                szm1, rx, sx, ry, sy, ux, uy, uz, vx, vy, vz, tx, ty, tz, qx, qy, qz, res, fin,
                loc, psem, s0, r0, s1, r1, s2, r2, s3, r3, s4, r4):
    z, xh, y, xl, core = [lax.axis_index(a) for a in DP_REP]
    x = xh * 2 + xl

    def at_x(i):
        return {"dp_1": lax.div(i, 2), "rep_0": lax.rem(i, 2)}

    def at_y(i):
        return {"dp_2": i}

    def at_z(i):
        return {"dp_0": i}

    partner = {"rep_1": 1 - core}

    loads = [(tok.at[2], cand_t.at[0]), (tok_a, cand_t.at[1]), (tok_b, cand_t.at[2])]
    loads += [(cot.at[2], cand_c.at[0]), (cot_a, cand_c.at[1]), (cot_b, cand_c.at[2])]
    loads = [pltpu.make_async_copy(a, b, loc.at[i]) for i, (a, b) in enumerate(loads)]
    for load in loads[:3]:
        load.start()
    for k in range(SLABS):
        slab_copy(proj, proj_v, psem, k).start()
    for load in loads[3:]:
        load.start()

    barrier = pltpu.get_barrier_semaphore()
    peers = [partner]
    peers += [at_x(wrap(x + d, NX)) for d in range(1, NX)]
    peers += [at_y(wrap(y + d, NY)) for d in range(1, NY)]
    peers += [at_z(wrap(z + d, NZ)) for d in range(1, NZ)]
    for peer in peers:
        pl.semaphore_signal(barrier, inc=1, device_id=peer, device_id_type=MESH)

    sent = []

    def send(src, dst, ss, rs, dev):
        copy = pltpu.make_async_remote_copy(
            src_ref=src, dst_ref=dst, send_sem=ss, recv_sem=rs, device_id=dev, device_id_type=MESH
        )
        copy.start()
        sent.append(copy)
        return copy

    def add(*refs):
        total = refs[0][...].astype(F32)
        for ref in refs[1:]:
            total = total + ref[...].astype(F32)
        return total

    def chosen(c):
        way = jnp.broadcast_to(info[1:2, 0:1], c.shape[1:])
        return jnp.where(way == 1, c[1], jnp.where(way == 2, c[2], c[0]))

    for load in loads[:3]:
        load.wait()
    x3[...] = chosen(cand_t)
    for r in range(D // 512):
        xt3[r * 512 : (r + 1) * 512, :] = x3[:, r * 512 : (r + 1) * 512].T
    join(proj, proj_v, psem, x3, acc3, joined3)
    for load in loads[3:]:
        load.wait()
    up3[...] = chosen(cand_c)
    attention(slice(None), info[2:3, 0:1], joined3, up3, comb3)
    pl.semaphore_wait(barrier, len(peers))

    tile, chunk = 128, 512
    other = 1 - core

    def step(begin, end):
        if begin is not None:
            j, to_partner, buf = begin
            cols = pl.ds(pl.multiple_of(((other if to_partner else core) * 3 + j) * HS, HS), HS)

        total = jnp.zeros((8, HS), F32)
        for q in range(D // chunk):
            if begin is not None:
                at = pl.ds(q * chunk, chunk)
                new = dot(xt01[at, :], comb01[:, cols], 1, 0)
                new = new + dot(xt3[at, :], comb3[:, cols], 1, 0)
                grad[buf, at, :] = new
                total = total + jnp.sum((new * new).reshape(chunk // 8, 8, HS), axis=0)
            if end is None:
                continue
            for t in range(chunk // tile):
                a, h = divmod(q * (chunk // tile) + t, 2)
                old = grad[end[2], pl.ds(a * 256 + h * tile, tile), :]
                soft = (old / (jnp.abs(old) + end[3])).reshape(NY, 2, 16, HS)
                if end[1]:
                    mail[end[0], a, h] = soft.astype(BF16)
                    continue
                both = (soft + part[end[0], a, h].astype(F32)).astype(BF16)
                if end[0] == 0:
                    wz[a, h] = both
                elif end[0] == 1:
                    for l in range(2):
                        wx[h, l, a] = both[:, l]
                else:
                    for b in range(NY):
                        wy[b, a, h] = both[b]
        if begin is None:
            return None
        total = jnp.sum(jnp.sum(total, axis=0, keepdims=True), axis=1, keepdims=True)
        return (*begin, 0.25 * jnp.sqrt(total * (1.0 / (D * HS)) + 1e-06))

    first = {}

    def post(j):
        first[j] = send(mail.at[j], part.at[j], s0.at[j], r0.at[j], partner)

    now = step((0, True, 0), None)
    now = step((1, True, 1), now)
    post(0)
    now = step((2, True, 0), now)
    post(1)
    now = step((0, False, 1), now)
    post(2)
    first[0].wait_recv()
    now = step((1, False, 0), now)

    up_z, down_z = at_z(wrap(z + 1, NZ)), at_z(wrap(z - 1, NZ))

    def zpiece(d, h):
        return wz.at[wrap(z + d, NZ), h]

    zp0 = [send(zpiece(4, 0), rzp0.at[0], s1.at[0], r1.at[0], up_z)]
    zm1 = [send(zpiece(-4, 1), rzm1.at[0], s1.at[1], r1.at[1], down_z)]
    zp1 = [send(zpiece(3, 1), rzp1.at[0], s1.at[2], r1.at[2], up_z)]
    zm0 = [send(zpiece(-3, 0), rzm0.at[0], s1.at[3], r1.at[3], down_z)]

    def four_ring(j, c, w, dev, recv, base):
        ahead, behind = dev(wrap(c + 1, 4)), dev(wrap(c - 1, 4))
        far = wrap(c + 2, 4)
        lo, hi = pl.ds(0, 4), pl.ds(4, 4)
        sem = lambda i: (s2.at[base + i], r2.at[base + i])
        return [
            send(w(far).at[lo], recv.at[0], *sem(0), ahead),
            send(w(far).at[hi], recv.at[1], *sem(1), behind),
            send(w(wrap(c + 1, 4)).at[hi], recv.at[3], *sem(2), ahead),
            send(w(wrap(c - 1, 4)).at[lo], recv.at[4], *sem(3), behind),
        ]

    def relay(c, w, dev, recv, hold, base, begun):
        ahead, behind = dev(wrap(c + 1, 4)), dev(wrap(c - 1, 4))
        sem = lambda i: (s2.at[base + i], r2.at[base + i])
        out_copies = []
        for i, (step, half, slot, to) in enumerate(((1, 0, 2, ahead), (-1, 4, 5, behind))):
            begun[i].wait_recv()
            mine = w(wrap(c + step, 4))

            @pl.loop(0, 4)
            def _(a):
                hold[i, a] = add(mine.at[half + a], recv.at[i, a]).astype(BF16)

            out_copies.append(send(hold.at[i], recv.at[slot], *sem(4 + i), to))
        return out_copies

    wx_of = lambda c: wx.at[lax.div(c, 2), lax.rem(c, 2)]
    wy_of = lambda c: wy.at[c]

    first[1].wait_recv()
    now = step((2, False, 1), now)
    bx = four_ring(1, x, wx_of, at_x, rx, 0)
    first[2].wait_recv()
    step(None, now)
    by = four_ring(2, y, wy_of, at_y, ry, 6)

    def z_relay(k):
        def hop(chain, recv, hold, d, h, sem, to):
            chain[k - 1].wait_recv()
            hold[k - 1] = add(zpiece(d, h), recv.at[k - 1]).astype(BF16)
            chain.append(send(hold.at[k - 1], recv.at[k], s1.at[sem], r1.at[sem], to))

        hop(zp0, rzp0, szp0, 4 - k, 0, 4 * k, up_z)
        hop(zm1, rzm1, szm1, k - 4, 1, 4 * k + 1, down_z)
        if k < 3:
            hop(zp1, rzp1, szp1, 3 - k, 1, 4 * k + 2, up_z)
            hop(zm0, rzm0, szm0, k - 3, 0, 4 * k + 3, down_z)

    z_relay(1)
    cx = relay(x, wx_of, at_x, rx, sx, 0, bx)
    cy = relay(y, wy_of, at_y, ry, sy, 6, by)
    z_relay(2)
    z_relay(3)

    def settle(c, w, recv, begun, later, store):
        later[0].wait_recv()
        begun[2].wait_recv()
        begun[3].wait_recv()
        later[1].wait_recv()
        mine = w(c)

        @pl.loop(0, 4)
        def _(a):
            store(a, add(mine.at[a], recv.at[2, a], recv.at[4, a]))
            store(4 + a, add(mine.at[4 + a], recv.at[3, a], recv.at[5, a]))

    def store_x(a, v):
        ux[:, a] = v.astype(BF16)

    def store_y(a, v):
        uy[:, :, a] = v.astype(BF16)

    def spread(u, c, n, dev, recv, ss, rs, base):
        return [
            send(u(wrap(c + d, n)), recv.at[d - 1], ss.at[base + d - 1], rs.at[base + d - 1],
                 dev(wrap(c + d, n)))
            for d in range(1, n)
        ]

    ux_of = lambda c: ux.at[c]
    uy_of = lambda c: uy.at[lax.div(c, 2), lax.rem(c, 2)]
    uz_of = lambda c: uz.at[lax.div(c, 2), lax.rem(c, 2)]
    settle(x, wx_of, rx, bx, cx, store_x)
    dx = spread(ux_of, y, NY, at_y, vx, s3, r3, 0)
    settle(y, wy_of, ry, by, cy, store_y)
    dy = spread(uy_of, x, NX, at_x, vy, s3, r3, 3)
    for chain in (zp0, zm0, zp1, zm1):
        chain[-1].wait_recv()
    for h, (a, b) in enumerate(((rzp0.at[3], rzm0.at[2]), (rzp1.at[2], rzm1.at[3]))):
        v = add(zpiece(0, h), a, b)
        for l in range(2):
            uz[h, l] = v[:, l].astype(BF16)
    dz = spread(uz_of, x, NX, at_x, vz, s3, r3, 6)

    def gather(copies, u, c, recv, hold):
        for copy in copies:
            copy.wait_recv()
        hold[...] = add(u(c), *[recv.at[i] for i in range(len(copies))]).astype(BF16)

    gather(dx, ux_of, y, vx, tx)
    ex = spread(lambda c: tx.at[c], z, NZ, at_z, qx, s4, r4, 0)
    gather(dy, uy_of, x, vy, ty)
    ey = spread(lambda c: ty.at[c], z, NZ, at_z, qy, s4, r4, 7)
    gather(dz, uz_of, x, vz, tz)
    ez = spread(lambda c: tz.at[c], y, NY, at_y, qz, s4, r4, 14)

    def finish(j, copies, mine, recv):
        for copy in copies:
            copy.wait_recv()
        total = add(mine, *[recv.at[i] for i in range(len(copies))]) * (1.0 / 16.0)
        res[j, 0] = total[0:8]
        res[j, 1] = total[8:16]

    finish(0, ez, tz.at[y], qz)
    finish(1, ex, tx.at[z], qx)
    finish(2, ey, ty.at[z], qy)
    ends = [
        send(res.at[j, 1 - core], fin.at[j], s0.at[3 + j], r0.at[3 + j], partner) for j in range(3)
    ]
    for j in range(3):
        out[core * 3 + j] = res[j, core]
    for j in range(3):
        ends[j].wait_recv()
        out[(1 - core) * 3 + j] = fin[j]
    for copy in sent:
        copy.wait_send()


def vote_sum(info, tokens, cotangent, moved, projection, comb, xt):
    vmem = pltpu.VMEM
    t = (16, HS)
    bf = lambda *dims: vmem(dims + t, BF16)
    sems = lambda n: pltpu.SemaphoreType.DMA((n,))
    scratch = [
        vmem((3, BLOCK, D), BF16),
        vmem((3, BLOCK, HEADS * HS), BF16),
        vmem((D, GROUPS * HS), BF16),
        vmem((BLOCK, D), BF16),
        vmem((BLOCK, HEADS * HS), BF16),
        vmem((BLOCK, GROUPS * HS), F32),
        vmem((BLOCK, GROUPS * HS), BF16),
        vmem((BLOCK, GROUPS * HS), BF16),
        vmem((D, BLOCK), BF16),
        vmem((2, D, HS), F32),
        bf(3, 8, 2, 4, 2),
        bf(3, 8, 2, 4, 2),
        bf(8, 2, 4, 2),
        bf(2, 2, 8, 4),
        bf(4, 8, 2, 2),
        bf(4, 4, 2), bf(3, 4, 2), bf(3, 4, 2), bf(4, 4, 2),
        bf(3, 4, 2), bf(2, 4, 2), bf(2, 4, 2), bf(3, 4, 2),
        bf(6, 4, 4), bf(2, 4, 4),
        bf(6, 4, 2, 2), bf(2, 4, 2, 2),
        bf(4, 8), bf(2, 2, 8), bf(2, 2, 4),
        bf(3, 8), bf(3, 8), bf(3, 4),
        bf(8), bf(8), bf(4),
        bf(7), bf(7), bf(3),
        vmem((3, 2, 8, HS), F32),
        vmem((3, 8, HS), F32),
        sems(6), sems(SLABS),
        sems(6), sems(6), sems(16), sems(16), sems(12), sems(12), sems(9), sems(9), sems(17), sems(17),
    ]
    return pl.pallas_call(
        vote_kernel,
        out_shape=jax.ShapeDtypeStruct((GROUPS, 8, HS), F32),
        in_specs=[pl.BlockSpec(memory_space=vmem)]
        + [pl.BlockSpec(memory_space=pl.ANY)] * 7
        + [pl.BlockSpec(memory_space=vmem)] * 2,
        out_specs=pl.BlockSpec(memory_space=pltpu.VMEM),
        scratch_shapes=scratch,
        compiler_params=pltpu.CompilerParams(
            collective_id=1, has_side_effects=True, vmem_limit_bytes=52 << 20
        ),
        name="vote_sum",
    )(info, tokens, cotangent, *moved, projection, comb, xt)


LEVELS = 6
PAIRS = [(a, b) for a in range(LEVELS) for b in range(a + 1, LEVELS)]
ALONE = {0: (0, 2), 1: (1, 2), 2: (0, 2), 3: (2, 3), 4: (2, 4), 5: (2, 5)}
APART = [((0, 1), (2, 3, 4, 5)), ((3, 4), (0, 1, 2, 5)), ((3, 5), (0, 1, 2, 4)), ((4, 5), (0, 1, 2))]
APART += [((n, 4), (3,)) for n in range(3)] + [((n, 5), (4,)) for n in range(3)]
APART = [(a, b, c, v) for (a, b), bits in APART for c in bits for v in range(2)]


def flipped(i, m):
    return i + m - 2 * m * lax.rem(lax.div(i, m), 2)


def across(level):
    if level < 2:
        return {"dp_2": flipped(lax.axis_index("dp_2"), 1 << level)}
    if level == 2:
        return {"dp_1": 1 - lax.axis_index("dp_1")}
    return {"dp_0": flipped(lax.axis_index("dp_0"), 1 << (level - 3))}


def plan_kernel(dest, lengths, tok, cot, proj, info, comb, xt, x01, up01, proj_v, acc, joined,
                mine, mixed, from_plane, from_z, loc, psem, ss, rs):
    z, xh, y, xl, core = [lax.axis_index(a) for a in DP_REP]
    x = xh * 2 + xl

    def at_plane(dx, dy, c):
        i = wrap(x + dx, NX)
        return {"dp_1": lax.div(i, 2), "rep_0": lax.rem(i, 2), "dp_2": wrap(y + dy, NY), "rep_1": c}

    plane = [(dx, dy, c) for dx in range(NX) for dy in range(NY) for c in range(2)][1:]
    plane = [at_plane(dx, dy, 1 - core if c else core) for dx, dy, c in plane]
    column = [{"dp_0": wrap(z + d, NZ)} for d in range(1, NZ)]
    peers = plane + column

    halves = [pl.ds(0, BLOCK), pl.ds(BLOCK, BLOCK)]
    loads = [(tok.at[b], x01.at[halves[b]]) for b in range(2)]
    loads += [(cot.at[b], up01.at[halves[b]]) for b in range(2)]
    loads = [pltpu.make_async_copy(a, b, loc.at[i]) for i, (a, b) in enumerate(loads)]
    for load in loads[:2]:
        load.start()
    for k in range(SLABS):
        slab_copy(proj, proj_v, psem, k).start()
    for load in loads[2:]:
        load.start()

    barrier = pltpu.get_barrier_semaphore()
    for peer in peers:
        pl.semaphore_signal(barrier, inc=1, device_id=peer, device_id_type=MESH)

    here = (xh * NY + y) * 4 + xl * 2 + core
    rank = z * 8 + xh * NY + y
    wide = (1, 128)
    lane = lax.broadcasted_iota(jnp.int32, wide, 1)
    target = jnp.full(wide, dest[0], jnp.int32)
    code = jnp.zeros(wide, jnp.int32)
    for level in range(LEVELS):
        code = jnp.where(target == flipped(rank, 1 << level), level + 1, code)
    code = code * 256 + jnp.full(wide, lengths[3], jnp.int32)
    mine[...] = jnp.where((lane == here) & (target >= 0), code, 0)

    for load in loads[:2]:
        load.wait()

    def spread(src, stage, landing, base):
        copies = []
        for i, peer in enumerate(stage):
            copy = pltpu.make_async_remote_copy(
                src_ref=src, dst_ref=landing.at[i], send_sem=ss.at[base + i],
                recv_sem=rs.at[base + i], device_id=peer, device_id_type=MESH,
            )
            copy.start()
            copies.append(copy)
        return copies

    pl.semaphore_wait(barrier, len(peers))
    first = spread(mine, plane, from_plane, 0)
    join(proj, proj_v, psem, x01, acc, joined)
    for load in loads[2:]:
        load.wait()
    for copy in first:
        copy.wait_recv()
    row = mine[...]
    for i in range(len(plane)):
        row = jnp.maximum(row, from_plane[i])
    mixed[...] = row
    second = spread(mixed, column, from_z, len(plane))
    for b in range(2):
        attention(halves[b], lengths[b], joined, up01, comb)
    for r in range(D // 512):
        xt[r * 512 : (r + 1) * 512, :] = x01[:, r * 512 : (r + 1) * 512].T
    for copy in second:
        copy.wait_recv()

    shape = (8, 128)
    behind = lax.broadcasted_iota(jnp.int32, shape, 0)
    lane = lax.broadcasted_iota(jnp.int32, shape, 1)
    table = jnp.broadcast_to(mixed[...], shape)
    for k in range(1, NZ):
        table = jnp.where(behind == k, jnp.broadcast_to(from_z[k - 1], shape), table)
    level_of = lax.shift_right_logical(table, 8)

    def largest(v):
        v = v.astype(F32)
        return jnp.max(jnp.max(v, axis=1, keepdims=True), axis=0, keepdims=True)

    active = jnp.zeros((1, 1), F32)
    sender = jnp.zeros(shape, jnp.int32)
    for level in range(LEVELS):
        found = level_of == level + 1
        active += largest(jnp.where(found, 1 << level, 0))
        if level < 2:
            there, back = here + (flipped(y, 1 << level) - y) * 4, z * 0
        elif level == 2:
            there, back = here + (1 - 2 * xh) * NY * 4, z * 0
        else:
            there, back = here, wrap(z - flipped(z, 1 << (level - 3)), NZ)
        sender = jnp.where(found & (lane == there) & (behind == back), table, sender)
    inbound = largest(lax.shift_right_logical(sender, 8))
    arriving = largest(jnp.bitwise_and(sender, 255))
    third = jnp.where(inbound > 0.0, arriving, jnp.full((1, 1), lengths[2], jnp.int32).astype(F32))
    branch = jnp.full((1, 1), float(len(PAIRS)), F32)
    way = jnp.ones((1, 1), F32)
    for p, (a, b) in enumerate(PAIRS):
        sets = [(1 << a) + (1 << b)] + [1 << s for s, both in ALONE.items() if both == (a, b)]
        hit = active == float(sets[0])
        for other in sets[1:] + ([0] if p == 0 else []):
            hit = hit | (active == float(other))
        branch = jnp.where(hit, float(p), branch)
        by = jnp.where(inbound == a + 1.0, 1.0, jnp.where(inbound == b + 1.0, 2.0, 0.0))
        way = jnp.where(hit, by, way)
    zrow = wrap(z - behind, NZ)
    ranks = zrow * 8 + lax.div(lane, 4)

    def has(level, c, v):
        bit = jnp.bitwise_and(lax.shift_right_logical(ranks, c), 1)
        return largest(jnp.where((level_of == level + 1) & (bit == v), 1, 0))

    seen = {(a, c, v): has(a, c, v) for a, c, v in sorted({(l, c, v) for a, b, c, _ in APART
                                                           for l in (a, b) for v in range(2)})}
    for p, (a, b, c, v) in enumerate(APART):
        clear = seen[a, c, 1 - v] + seen[b, c, v] == 0.0
        clear = clear & (active == float((1 << a) + (1 << b)))
        branch = jnp.where(clear, float(len(PAIRS) + 1 + p), branch)
        way = jnp.where(clear, jnp.where(inbound > 0.0, 1.0, 0.0), way)
    told = jnp.zeros(shape, F32)
    for i, v in enumerate((branch, way, third, inbound, active)):
        told = jnp.where(behind == i, v, told)
    info[...] = told.astype(jnp.int32)
    for copy in first + second:
        copy.wait_send()


def plan(destination, lengths, tokens, cotangent, projection):
    vmem = pltpu.VMEM
    plane, column = 2 * NX * NY - 1, NZ - 1
    width = GROUPS * HS
    return pl.pallas_call(
        plan_kernel,
        out_shape=(
            jax.ShapeDtypeStruct((8, 128), jnp.int32),
            jax.ShapeDtypeStruct((2 * BLOCK, width), BF16),
            jax.ShapeDtypeStruct((D, 2 * BLOCK), BF16),
        ),
        in_specs=[pl.BlockSpec(memory_space=pltpu.SMEM)] * 2
        + [pl.BlockSpec(memory_space=pltpu.HBM)] * 3,
        out_specs=[pl.BlockSpec(memory_space=vmem)] * 3,
        scratch_shapes=[
            vmem((2 * BLOCK, D), BF16),
            vmem((2 * BLOCK, HEADS * HS), BF16),
            vmem((D, width), BF16),
            vmem((2 * BLOCK, width), F32),
            vmem((2 * BLOCK, width), BF16),
            vmem((1, 128), jnp.int32),
            vmem((1, 128), jnp.int32),
            vmem((plane, 1, 128), jnp.int32),
            vmem((column, 1, 128), jnp.int32),
            pltpu.SemaphoreType.DMA((4,)),
            pltpu.SemaphoreType.DMA((SLABS,)),
            pltpu.SemaphoreType.DMA((plane + column,)),
            pltpu.SemaphoreType.DMA((plane + column,)),
        ],
        compiler_params=pltpu.CompilerParams(
            collective_id=2, has_side_effects=True, vmem_limit_bytes=52 << 20
        ),
        name="plan",
    )(destination, lengths, tokens, cotangent, projection)


def move_apart(p):
    a, b, c, v = APART[p]

    def kernel(tokens, cotangent, tok_a, cot_a, tok_b, cot_b, ss, rs):
        here = {name: lax.axis_index(name) for name in DP}
        rank = (here["dp_0"] * 2 + here["dp_1"]) * NY + here["dp_2"]
        bit = lax.rem(lax.div(rank, 1 << c), 2)
        in_a = bit if v else 1 - bit
        to_a, to_b = {**here, **across(a)}, {**here, **across(b)}
        peer = {name: to_b[name] + in_a * (to_a[name] - to_b[name]) for name in DP}
        barrier = pltpu.get_barrier_semaphore()
        pl.semaphore_signal(barrier, inc=1, device_id=peer, device_id_type=MESH)
        pl.semaphore_wait(barrier, 1)
        copies = []
        for i, (src, dst) in enumerate(((tokens, tok_a), (cotangent, cot_a))):
            copies.append(pltpu.make_async_remote_copy(
                src_ref=src.at[3], dst_ref=dst, send_sem=ss.at[i], recv_sem=rs.at[i],
                device_id=peer, device_id_type=MESH,
            ))
            copies[-1].start()
        for copy in copies:
            copy.wait()

    return mover(kernel, 3 + len(PAIRS) + p)


def move_pair(p):
    peers_of = PAIRS[p]

    def kernel(tokens, cotangent, tok_a, cot_a, tok_b, cot_b, ss, rs):
        peers = [across(level) for level in peers_of]
        barrier = pltpu.get_barrier_semaphore()
        for peer in peers:
            pl.semaphore_signal(barrier, inc=1, device_id=peer, device_id_type=MESH)
        pl.semaphore_wait(barrier, 2)
        copies = []
        for i, (src, dst, peer) in enumerate((
            (tokens, tok_a, peers[0]), (tokens, tok_b, peers[1]),
            (cotangent, cot_a, peers[0]), (cotangent, cot_b, peers[1]),
        )):
            copies.append(pltpu.make_async_remote_copy(
                src_ref=src.at[3], dst_ref=dst, send_sem=ss.at[i], recv_sem=rs.at[i],
                device_id=peer, device_id_type=MESH,
            ))
            copies[-1].start()
        for copy in copies:
            copy.wait()

    return mover(kernel, 3 + p)


def mover(kernel, collective_id):
    def call(tokens, cotangent, info):
        block = jax.ShapeDtypeStruct(tokens.shape[1:], BF16)
        upstream = jax.ShapeDtypeStruct(cotangent.shape[1:], BF16)
        return pl.pallas_call(
            kernel,
            out_shape=(block, upstream, block, upstream),
            in_specs=[pl.BlockSpec(memory_space=pl.ANY)] * 2,
            out_specs=[pl.BlockSpec(memory_space=pl.ANY)] * 4,
            scratch_shapes=[pltpu.SemaphoreType.DMA((4,)), pltpu.SemaphoreType.DMA((4,))],
            compiler_params=pltpu.CompilerParams(
                collective_id=collective_id, has_side_effects=True, vmem_limit_bytes=2 << 20
            ),
            name="move",
        )(tokens, cotangent)

    return call


def swapped(value, axis, apart):
    mask = 2**apart
    pairs = [(source, source ^ mask) for source in range(lax.axis_size(axis))]
    return lax.ppermute(value, axis, pairs)


def move_many(tokens, cotangent, info):
    kept = (tokens[2], cotangent[2])
    for level in range(LEVELS):

        def trade(kept, level=level):
            got = swapped((tokens[3], cotangent[3]), DP, level)
            arrived = info[3, 0] == level + 1
            return jax.tree.map(lambda new, old: jnp.where(arrived, new, old), got, kept)

        needed = jnp.bitwise_and(jnp.right_shift(info[4, 0], level), 1) == 1
        kept = lax.cond(needed, trade, lambda kept: kept, kept)
    return (*kept, *kept)


def shards(tokens, cotangent, projection, block_lengths, destination):
    lengths = block_lengths[0]
    info, comb, xt = plan(destination, lengths, tokens, cotangent, projection)
    branches = [move_pair(p) for p in range(len(PAIRS))] + [move_many]
    branches += [move_apart(p) for p in range(len(APART))]
    moved = lax.switch(info[0, 0], branches, tokens, cotangent, info)
    summed = vote_sum(info, tokens, cotangent, moved, projection, comb, xt)
    return summed.transpose(1, 0, 2).reshape(8, GROUPS * HS)


def solution(mesh):
    split = Mesh(mesh.devices.reshape(8, 2, 4, 2, 2), DP_REP)
    placed = (P(DP_REP, None, None), P(DP_REP, None, None), P(), P(DP_REP, None), P(DP_REP))
    return jax.shard_map(
        shards, mesh=split, in_specs=placed, out_specs=P(DP_REP, None), check_vma=False
    )
```

profile of v0, /device:TPU:1, one launch (start us, length us, event | category | flops | bytes accessed | tf_op | source)
XLA Modules:
  0.0 97.0 jit_solution(553295434721032868)
XLA Ops:
  0.7 0.0 copy-start
  0.7 0.6 copy-done
  1.3 0.0 copy-start.1
  1.3 0.0 copy-start.3
  1.3 19.8 %plan.1 = (s32[8,128]{1,0:T(8,128)S(1)}, bf16[256,1536]{1,0:T(8,128)(2,1)S(1)}, bf16[2048,256]{1,0:T(8,128)(2,1)S(1)}) custom-call(s32[1]{0:T(128)S(6)} %copy.263.dest, s32[4]{0:T(128)S(1)} %bitcast.46, bf16[4,128,2048]{2,1,0:T(8,128)(2,1)} %tok.3, bf16[4,128,1024]{2,1,0:T(8,128)(2,1)} %cot.3, bf16[2048,1536]{1,0:T(8,128)(2,1)} %proj.3), custom_call_target="tpu_custom_call" | custom-call | tf_op jit(solution)/shard_map/plan/pallas_call | solution.py:557
  21.2 0.5 slice.71
  22.3 0.0 copy-done.1
  22.3 0.0 copy-done.3
  22.4 30.6 %conditional.7 = ((bf16[128,2048]{1,0:T(8,128)(2,1)}, bf16[128,1024]{1,0:T(8,128)(2,1)}, bf16[128,2048]{1,0:T(8,128)(2,1)S(1)}, bf16[128,1024]{1,0:T(8,128)(2,1)})) conditional(s32[]{:T(128)} %bitcast.27, (bf16[4,128,2048]{2,1,0:T(8,128)(2,1)S(1)}, bf16[4,128,1024]{2,1,0:T(8,128)(2,1)S(1)}) %tuple.451, ...), branch_computations={%region_0.0_spmd, %region_1.0_spmd, %region_2.0_spmd, %region_3.0_... | conditional | flops 2359326 | bytes 54002968 | solution.py:684
  22.8 29.8 %move.111 = (bf16[128,2048]{1,0:T(8,128)(2,1)}, bf16[128,1024]{1,0:T(8,128)(2,1)}, bf16[128,2048]{1,0:T(8,128)(2,1)S(1)}, bf16[128,1024]{1,0:T(8,128)(2,1)}) custom-call(bf16[4,128,2048]{2,1,0:T(8,128)(2,1)S(1)} %get-tuple-element.476.tokens, bf16[4,128,1024]{2,1,0:T(8,128)(2,1)S(1)} %get-tuple-element.477.cotangent), custom_call_target="tpu_custom_call" | custom-call | tf_op jit(solution)/shard_map/cond/branch_55_fun/move/pallas_call | solution.py:644
  53.0 43.4 %vote_sum.1 = f32[6,8,256]{2,1,0:T(8,128)S(1)} custom-call(s32[8,128]{1,0:T(8,128)S(1)} %get-tuple-element.489.info, bf16[4,128,2048]{2,1,0:T(8,128)(2,1)} %tok.3, bf16[4,128,1024]{2,1,0:T(8,128)(2,1)S(1)} %copy-done.3, bf16[128,2048]{1,0:T(8,128)(2,1)} %get-tuple-element.490.tok_a, bf16[128,1024]{1,0:T(8,128)(2,1)} %get-tuple-element.491.cot_a, ...), custom_call_target="tpu_custom_call" | custom-call | tf_op jit(solution)/shard_map/vote_sum/pallas_call | solution.py:386
  96.4 0.6 copy.264
Async XLA Ops:
  0.7 0.7 copy-start
  1.3 21.0 %copy-start.1 = (bf16[4,128,2048]{2,1,0:T(8,128)(2,1)S(1)}, bf16[4,128,2048]{2,1,0:T(8,128)(2,1)}, u32[]{:S(2)}) copy-start(bf16[4,128,2048]{2,1,0:T(8,128)(2,1)} %tok.3) | copy-start | bytes 6291460
  1.3 21.0 %copy-start.3 = (bf16[4,128,1024]{2,1,0:T(8,128)(2,1)S(1)}, bf16[4,128,1024]{2,1,0:T(8,128)(2,1)}, u32[]{:S(2)}) copy-start(bf16[4,128,1024]{2,1,0:T(8,128)(2,1)} %cot.3) | copy-start | bytes 3145732
where the time goes:
time: 98.1 us; the launch traced here: 97 us
  Pallas kernels  93 us (95%)
  local copies, waits for them, and re-layouts  1.79 us (2%)
  between operations  1.36 us (1%)
    pallas_call x1, Pallas kernels, vote_sum(): pl.pallas_call(vote_kernel, out_shape=jax.ShapeDtypeStruct((GROUPS, 8, HS...  43.4 us
    pallas_call x1, Pallas kernels, call(): pl.pallas_call(kernel, out_shape=(block, upstream, block, upstream), in_s...  29.8 us
    pallas_call x1, Pallas kernels, plan(): pl.pallas_call(plan_kernel, out_shape=(jax.ShapeDtypeStruct((8, 128), jnp...  19.8 us

commit v1 on v0

--- a/solution.py
+++ b/solution.py
@@ -401,8 +401,8 @@
 LEVELS = 6
 PAIRS = [(a, b) for a in range(LEVELS) for b in range(a + 1, LEVELS)]
 ALONE = {0: (0, 2), 1: (1, 2), 2: (0, 2), 3: (2, 3), 4: (2, 4), 5: (2, 5)}
-APART = [((0, 1), (2, 3, 4, 5)), ((3, 4), (0, 1, 2, 5)), ((3, 5), (0, 1, 2, 4)), ((4, 5), (0, 1, 2))]
-APART += [((n, 4), (3,)) for n in range(3)] + [((n, 5), (4,)) for n in range(3)]
+APART = [((0, 1), (2, 3, 4, 5)), ((3, 5), (0, 1, 2)), ((4, 5), (0, 1, 2))]
+APART += [((n, 4), (3,)) for n in range(3)]
 APART = [(a, b, c, v) for (a, b), bits in APART for c in bits for v in range(2)]
 
 
@@ -656,24 +656,58 @@
     return call
 
 
-def swapped(value, axis, apart):
-    mask = 2**apart
-    pairs = [(source, source ^ mask) for source in range(lax.axis_size(axis))]
-    return lax.ppermute(value, axis, pairs)
+def many_kernel(info, tokens, cotangent, tok_a, cot_a, tok_b, cot_b, all_t, all_c, own, ss, rs):
+    peers = [across(level) for level in range(LEVELS)]
+    barrier = pltpu.get_barrier_semaphore()
+    for peer in peers:
+        pl.semaphore_signal(barrier, inc=1, device_id=peer, device_id_type=MESH)
+    keep = [
+        pltpu.make_async_copy(tokens.at[2], tok_a, own.at[0]),
+        pltpu.make_async_copy(cotangent.at[2], cot_a, own.at[1]),
+    ]
+    for copy in keep:
+        copy.start()
+    pl.semaphore_wait(barrier, LEVELS)
+    copies = []
+    for level, peer in enumerate(peers):
+        for i, (src, dst) in enumerate(((tokens, all_t), (cotangent, all_c))):
+            copies.append(pltpu.make_async_remote_copy(
+                src_ref=src.at[3], dst_ref=dst.at[level], send_sem=ss.at[2 * level + i],
+                recv_sem=rs.at[2 * level + i], device_id=peer, device_id_type=MESH,
+            ))
+            copies[-1].start()
+    for copy in keep:
+        copy.wait()
+    for copy in copies:
+        copy.wait()
+    for level in range(LEVELS):
+        for got, out in ((all_t, tok_a), (all_c, cot_a)):
+            arrived = jnp.broadcast_to(info[3:4, 0:1], out.shape) == level + 1
+            out[...] = jnp.where(arrived, got[level], out[...])
 
 
 def move_many(tokens, cotangent, info):
-    kept = (tokens[2], cotangent[2])
-    for level in range(LEVELS):
-
-        def trade(kept, level=level):
-            got = swapped((tokens[3], cotangent[3]), DP, level)
-            arrived = info[3, 0] == level + 1
-            return jax.tree.map(lambda new, old: jnp.where(arrived, new, old), got, kept)
-
-        needed = jnp.bitwise_and(jnp.right_shift(info[4, 0], level), 1) == 1
-        kept = lax.cond(needed, trade, lambda kept: kept, kept)
-    return (*kept, *kept)
+    block, upstream = tokens.shape[1:], cotangent.shape[1:]
+    like = [jax.ShapeDtypeStruct(s, BF16) for s in (block, upstream)]
+    vmem = pltpu.VMEM
+    return pl.pallas_call(
+        many_kernel,
+        out_shape=(*like, *like),
+        in_specs=[pl.BlockSpec(memory_space=vmem)] + [pl.BlockSpec(memory_space=pl.ANY)] * 2,
+        out_specs=[pl.BlockSpec(memory_space=vmem)] * 2 + [pl.BlockSpec(memory_space=pl.ANY)] * 2,
+        scratch_shapes=[
+            vmem((LEVELS,) + block, BF16),
+            vmem((LEVELS,) + upstream, BF16),
+            pltpu.SemaphoreType.DMA((2,)),
+            pltpu.SemaphoreType.DMA((2 * LEVELS,)),
+            pltpu.SemaphoreType.DMA((2 * LEVELS,)),
+        ],
+        compiler_params=pltpu.CompilerParams(
+            collective_id=3 + len(PAIRS) + len(APART), has_side_effects=True,
+            vmem_limit_bytes=10 << 20,
+        ),
+        name="move_many",
+    )(info, tokens, cotangent)
 
 
 def shards(tokens, cotangent, projection, block_lengths, destination):

time: 98.1 us -> 99.7 us (1.016); the launches traced: 97 us -> 100 us
  Pallas kernels: 93 us -> 96.7 us
    pallas_call x1, Pallas kernels: 29.8 us -> 37.2 us  [call(): pl.pallas_call(kernel, out_shape=(block, upstream, block, upstream), in_s...]
    pallas_call x1, Pallas kernels: 43.4 us -> 39.7 us  [vote_sum(): pl.pallas_call(vote_kernel, out_shape=jax.ShapeDtypeStruct((GROUPS, 8, HS...]
where the time goes in v1:
time: 99.7 us; the launch traced here: 100 us
  Pallas kernels  96.7 us (97%)
  local copies, waits for them, and re-layouts  1.79 us (2%)
  between operations  1.36 us (1%)
    pallas_call x1, Pallas kernels, vote_sum(): pl.pallas_call(vote_kernel, out_shape=jax.ShapeDtypeStruct((GROUPS, 8, HS...  39.7 us
    pallas_call x1, Pallas kernels, call(): pl.pallas_call(kernel, out_shape=(block, upstream, block, upstream), in_s...  37.2 us
    pallas_call x1, Pallas kernels, plan(): pl.pallas_call(plan_kernel, out_shape=(jax.ShapeDtypeStruct((8, 128), jnp...  19.8 us

profile of v1, /device:TPU:1, one launch (start us, length us, event | category | flops | bytes accessed | tf_op | source)
XLA Modules:
  0.0 100.1 jit_solution(16069395369490880188)
XLA Ops:
  0.7 0.0 copy-start
  0.7 0.6 copy-done
  1.3 0.0 copy-start.1
  1.3 0.0 copy-start.2
  1.3 19.8 %plan.1 = (s32[8,128]{1,0:T(8,128)S(1)}, bf16[256,1536]{1,0:T(8,128)(2,1)S(1)}, bf16[2048,256]{1,0:T(8,128)(2,1)S(1)}) custom-call(s32[1]{0:T(128)S(6)} %copy.175.dest, s32[4]{0:T(128)S(1)} %bitcast.6, bf16[4,128,2048]{2,1,0:T(8,128)(2,1)} %tok.3, bf16[4,128,1024]{2,1,0:T(8,128)(2,1)} %cot.3, bf16[2048,1536]{1,0:T(8,128)(2,1)} %proj.3), custom_call_target="tpu_custom_call" | custom-call | tf_op jit(solution)/shard_map/plan/pallas_call | solution.py:557
  21.2 0.5 slice.3
  22.3 0.0 copy-done.1
  22.3 0.0 copy-done.2
  22.3 37.5 %conditional.1 = ((bf16[128,2048]{1,0:T(8,128)(2,1)S(1)}, bf16[128,1024]{1,0:T(8,128)(2,1)}, bf16[128,2048]{1,0:T(8,128)(2,1)}, bf16[128,1024]{1,0:T(8,128)(2,1)})) conditional(s32[]{:T(128)} %bitcast.1, (bf16[4,128,2048]{2,1,0:T(8,128)(2,1)S(1)}, bf16[4,128,1024]{2,1,0:T(8,128)(2,1)S(1)}) %tuple.280, ...), branch_computations={%region_0.0_spmd, %region_1.0_spmd, %region_2.0_spmd, %region_3.0_... | conditional | bytes 8 | solution.py:718
  22.4 37.2 %move.74 = (bf16[128,2048]{1,0:T(8,128)(2,1)S(1)}, bf16[128,1024]{1,0:T(8,128)(2,1)}, bf16[128,2048]{1,0:T(8,128)(2,1)}, bf16[128,1024]{1,0:T(8,128)(2,1)}) custom-call(bf16[4,128,2048]{2,1,0:T(8,128)(2,1)S(1)} %get-tuple-element.244.tokens, bf16[4,128,1024]{2,1,0:T(8,128)(2,1)S(1)} %get-tuple-element.245.cotangent), custom_call_target="tpu_custom_call" | custom-call | tf_op jit(solution)/shard_map/cond/branch_34_fun/move/pallas_call | solution.py:644
  59.8 39.7 %vote_sum.1 = f32[6,8,256]{2,1,0:T(8,128)S(1)} custom-call(s32[8,128]{1,0:T(8,128)S(1)} %get-tuple-element.267.info, bf16[4,128,2048]{2,1,0:T(8,128)(2,1)} %tok.3, bf16[4,128,1024]{2,1,0:T(8,128)(2,1)S(1)} %copy-done.2, bf16[128,2048]{1,0:T(8,128)(2,1)S(1)} %get-tuple-element.268.tok_a, bf16[128,1024]{1,0:T(8,128)(2,1)} %get-tuple-element.269.cot_a, ...), custom_call_target="tpu_custom_call" | custom-call | tf_op jit(solution)/shard_map/vote_sum/pallas_call | solution.py:386
  99.5 0.6 copy.176
Async XLA Ops:
  0.7 0.7 copy-start
  1.3 21.0 %copy-start.1 = (bf16[4,128,2048]{2,1,0:T(8,128)(2,1)S(1)}, bf16[4,128,2048]{2,1,0:T(8,128)(2,1)}, u32[]{:S(2)}) copy-start(bf16[4,128,2048]{2,1,0:T(8,128)(2,1)} %tok.3) | copy-start | bytes 6291460
  1.3 21.0 %copy-start.2 = (bf16[4,128,1024]{2,1,0:T(8,128)(2,1)S(1)}, bf16[4,128,1024]{2,1,0:T(8,128)(2,1)}, u32[]{:S(2)}) copy-start(bf16[4,128,1024]{2,1,0:T(8,128)(2,1)} %cot.3) | copy-start | bytes 3145732
